TPU v7x, 32 devices: a whole 2x2x4 slice. The times are simulated.
32 devices in a mesh: band: 16 (over z, y, core), sub: 2 (over x).
Axes of the slice: x: 2, y: 2, z: 4, core: 2. Of those that a mesh axis runs over, the one named last changes fastest.
Arguments:
- land_values: bfloat16 [64, 524288], P(None, ('band', 'sub')), may hold values from -6 to 6
- area_weights: bfloat16 [4096, 128, 128], P(('band', 'sub')), may hold values from 0.0019989014 to 0.029907227
- land_mask: int32 [524288], P(('band', 'sub')), may hold values 0 or 1
- dest_band: int32 [4096, 1], P(('band', 'sub')), may hold values from 0 to 15; in each aligned block of 128 rows (0 to 127, 128 to 255, ...) at most 16 rows name the same one
- dest_tile: int32 [4096], P(('band', 'sub')), may hold values from 0 to 399
- ocean_mask: int32 [819200], P(('band', 'sub')), may hold values 0 or 1
Outputs:
- remapped: float32 [64, 819200], P(None, ('band', 'sub'))
Inputs may be any that keep to these rules, and one draw needn't show every extreme that they name: `dest_band`: each device's 128 blocks name any one band at most 16 times; in every draw some device names one band exactly 16 times.
All inputs are finite; a program needn't handle non-finite values. No bound on the sum of `land_mask` or of `ocean_mask` on one device may be relied on, other than what follows from the above.
Results may differ from a plain program's by a relative error of at most 0.005.
Values may be sent and summed in bfloat16 or wider, within the bound.
A program may use at most 128 MiB of HBM per device.

v0:
```python
import functools

import jax
import jax.numpy as jnp
from jax import lax
from jax.experimental import pallas as pl
from jax.experimental.pallas import tpu as pltpu
from jax.sharding import PartitionSpec as P

cover_floor = 0.5
ROWS = 8
LANES = 128
MESH = pl.DeviceIdType.MESH


def target_of(me, k, bands):
    if bands & (bands - 1):
        return lax.rem(me + k, bands)
    peer, bit = 0, 1
    while bit < bands:
        peer = peer + bit * lax.rem(me // bit + k // bit, 2)
        bit *= 2
    return peer


def greet_bands(barrier, me, bands):
    @pl.loop(1, bands)
    def _(k):
        pl.semaphore_signal(
            barrier, inc=1, device_id={"band": target_of(me, k, bands)}, device_id_type=MESH
        )


def block_kernel(
    group, chunks, bands, v_ref, w_ref, m_ref, t_ref, p_ref, c_ref, r_ref,
    landed, send_sem, recv_sem,
):
    me = lax.axis_index("band")
    cells = w_ref.shape[1]

    def index_copy(k):
        d = target_of(me, k, bands)
        return pltpu.make_async_remote_copy(
            src_ref=t_ref.at[d], dst_ref=landed.at[k],
            send_sem=send_sem.at[k], recv_sem=recv_sem.at[k],
            device_id={"band": d}, device_id_type=MESH,
        )

    @pl.when(pl.program_id(0) == 0)
    def _():
        barrier = pltpu.get_barrier_semaphore()
        greet_bands(barrier, me, bands)
        pl.semaphore_wait(barrier, bands - 1)

        @pl.loop(1, bands)
        def _(k):
            index_copy(k).start()

    for j in range(group):
        lanes = pl.ds(j * cells, cells)
        mb = m_ref[:, lanes].astype(jnp.float32).astype(jnp.bfloat16)
        lhs = jnp.concatenate(
            [v_ref[:, lanes] * mb, jnp.broadcast_to(mb, (16, cells))], axis=0
        )
        p = jnp.dot(lhs, w_ref[j], preferred_element_type=jnp.float32)
        for c in range(chunks):
            p_ref[c, j] = p[c * ROWS:(c + 1) * ROWS].astype(jnp.bfloat16)
        c_ref[pl.ds(j, 1), :] = (
            p[chunks * ROWS:chunks * ROWS + 1].astype(jnp.bfloat16).astype(jnp.float32)
        )

    @pl.when(pl.program_id(0) == pl.num_programs(0) - 1)
    def _():
        @pl.loop(1, bands)
        def _(k):
            index_copy(k).wait_send()
            index_copy(k).wait_recv()

        r_ref[0] = t_ref[me]
        r_ref[pl.ds(1, bands - 1)] = landed[pl.ds(1, bands - 1)]


def block_products(bands, values, weights, mask, tile_sent):
    fields = values.shape[0]
    blocks, cells, out_cells = weights.shape
    chunks = fields // ROWS
    group = 16
    return pl.pallas_call(
        functools.partial(block_kernel, group, chunks, bands),
        grid=(blocks // group,),
        in_specs=[
            pl.BlockSpec((fields, group * cells), lambda i: (0, i)),
            pl.BlockSpec((group, cells, out_cells), lambda i: (i, 0, 0)),
            pl.BlockSpec((1, group * cells), lambda i: (0, i)),
            pl.BlockSpec(memory_space=pltpu.VMEM),
        ],
        out_specs=[
            pl.BlockSpec((chunks, group, ROWS, out_cells), lambda i: (0, i, 0, 0)),
            pl.BlockSpec((group, out_cells), lambda i: (i, 0)),
            pl.BlockSpec(memory_space=pltpu.VMEM),
        ],
        out_shape=[
            jax.ShapeDtypeStruct((chunks, blocks, ROWS, out_cells), jnp.bfloat16),
            jax.ShapeDtypeStruct((blocks, out_cells), jnp.float32),
            jax.ShapeDtypeStruct(tile_sent.shape, jnp.int32),
        ],
        scratch_shapes=[
            pltpu.VMEM(tile_sent.shape, jnp.int32),
            pltpu.SemaphoreType.DMA((bands,)),
            pltpu.SemaphoreType.DMA((bands,)),
        ],
        compiler_params=pltpu.CompilerParams(collective_id=1, has_side_effects=True),
        name="block_products",
    )(values, weights, mask, tile_sent)


def exchange_kernel(
    bands, cap, chunks, tiles,
    src_ref, prev_ref, last_ref, p_ref, c_ref, wet_ref, out_ref,
    send, recv, csend, crecv, run, crun, xsend, xrecv, cxsend, cxrecv, done,
    send_sem, recv_sem, csend_sem, crecv_sem, xsend_sem, xrecv_sem, out_sem,
):
    me = lax.axis_index("band")
    half = lax.axis_index("sub")
    slots = bands * cap
    cells = xsend.shape[3]
    other = {"sub": 1 - half}
    step = 8

    barrier = pltpu.get_barrier_semaphore()
    greet_bands(barrier, me, bands)
    pl.semaphore_signal(barrier, inc=1, device_id=other, device_id_type=MESH)
    pl.semaphore_wait(barrier, bands)

    def chunk_copy(c, k):
        return pltpu.make_async_remote_copy(
            src_ref=send.at[c, k], dst_ref=recv.at[c, k],
            send_sem=send_sem.at[c, k], recv_sem=recv_sem.at[c, k],
            device_id={"band": target_of(me, k, bands)}, device_id_type=MESH,
        )

    def cover_copy(k):
        return pltpu.make_async_remote_copy(
            src_ref=csend.at[k], dst_ref=crecv.at[k],
            send_sem=csend_sem.at[k], recv_sem=crecv_sem.at[k],
            device_id={"band": target_of(me, k, bands)}, device_id_type=MESH,
        )

    def half_copy(c):
        return pltpu.make_async_remote_copy(
            src_ref=xsend.at[c], dst_ref=xrecv.at[c],
            send_sem=xsend_sem.at[c], recv_sem=xrecv_sem.at[c],
            device_id=other, device_id_type=MESH,
        )

    half_cover = pltpu.make_async_remote_copy(
        src_ref=cxsend, dst_ref=cxrecv,
        send_sem=xsend_sem.at[chunks], recv_sem=xrecv_sem.at[chunks],
        device_id=other, device_id_type=MESH,
    )

    def out_copy(c):
        return pltpu.make_async_copy(
            done.at[c % 2], out_ref.at[pl.ds(c * ROWS, ROWS), :], out_sem.at[c % 2]
        )

    def each_tile(body):
        @pl.loop(0, tiles // step)
        def _(g):
            for u in range(step):
                body(g * step + u)

    def finish(c):
        half_copy(c).wait_recv()
        if c >= 2:
            out_copy(c - 2).wait()

        def one(t):
            total = run[c, last_ref[tiles + t]] + xrecv[c, t].astype(jnp.float32)
            lanes = pl.ds(pl.multiple_of(t * cells, cells), cells)
            done[c % 2, :, lanes] = total * cxrecv[pl.ds(t, 1), :]

        each_tile(one)
        out_copy(c).start()

    def send_chunk(c):
        @pl.loop(1, bands)
        def _(k):
            d = target_of(me, k, bands)
            for j in range(cap):
                send[c, k, j] = p_ref[c, src_ref[d * cap + j]]
            chunk_copy(c, k).start()

        for j in range(cap):
            recv[c, 0, j] = p_ref[c, src_ref[me * cap + j]]

    send_chunk(0)

    @pl.loop(1, bands)
    def _(k):
        d = target_of(me, k, bands)
        for j in range(cap):
            csend[k, pl.ds(j, 1), :] = c_ref[pl.ds(src_ref[d * cap + j], 1), :]
        cover_copy(k).start()

    for j in range(cap):
        crecv[0, pl.ds(j, 1), :] = c_ref[pl.ds(src_ref[me * cap + j], 1), :]

    for c in range(1, chunks):
        send_chunk(c)

    for c in range(chunks):
        run[c, slots] = jnp.zeros(run.shape[2:], jnp.float32)

        def add(k, c=c):
            for j in range(cap):
                i = k * cap + j
                run[c, i] = run[c, prev_ref[i]] + recv[c, k, j].astype(jnp.float32)

        add(0)

        @pl.loop(1, bands)
        def _(k, c=c):
            chunk_copy(c, k).wait_recv()
            add(k)

        def give(t, c=c):
            xsend[c, t] = run[c, last_ref[t]].astype(jnp.bfloat16)

        each_tile(give)
        half_copy(c).start()

        if c == 0:
            @pl.loop(1, bands)
            def _(k):
                cover_copy(k).wait_recv()

            crun[pl.ds(slots, 8), :] = jnp.zeros((8, cells), jnp.float32)

            @pl.loop(0, bands)
            def _(k):
                for j in range(cap):
                    i = k * cap + j
                    crun[pl.ds(i, 1), :] = (
                        crun[pl.ds(prev_ref[i], 1), :] + crecv[k, pl.ds(j, 1), :]
                    )

            def give_cover(t):
                cxsend[pl.ds(t, 1), :] = crun[pl.ds(last_ref[t], 1), :]

            each_tile(give_cover)
            half_cover.start()

        if c == 1:
            half_cover.wait_recv()

            def factor(t):
                row = pl.ds(t, 1)
                total = crun[pl.ds(last_ref[tiles + t], 1), :] + cxrecv[row, :]
                wet = wet_ref[row, :].astype(jnp.float32)
                cxrecv[row, :] = wet / jnp.maximum(total, cover_floor)

            each_tile(factor)

        if c >= 1:
            finish(c - 1)

    finish(chunks - 1)

    half_cover.wait_send()
    for c in range(chunks):
        half_copy(c).wait_send()

    @pl.loop(1, bands)
    def _(k):
        cover_copy(k).wait_send()
        for c in range(chunks):
            chunk_copy(c, k).wait_send()

    for c in range(max(0, chunks - 2), chunks):
        out_copy(c).wait()


def exchange(bands, cap, src, prev, last, partial, covered, wet):
    chunks, _, rows, cells = partial.shape
    tiles = wet.shape[0]
    slots = bands * cap
    smem = pl.BlockSpec(memory_space=pltpu.SMEM)
    vmem = pl.BlockSpec(memory_space=pltpu.VMEM)
    bf16, f32 = jnp.bfloat16, jnp.float32
    dma = pltpu.SemaphoreType.DMA
    return pl.pallas_call(
        functools.partial(exchange_kernel, bands, cap, chunks, tiles),
        in_specs=[smem, smem, smem, vmem, vmem, vmem],
        out_specs=pl.BlockSpec(memory_space=pl.ANY),
        out_shape=jax.ShapeDtypeStruct((chunks * rows, tiles * cells), f32),
        scratch_shapes=[
            pltpu.VMEM((chunks, bands, cap, rows, cells), bf16),
            pltpu.VMEM((chunks, bands, cap, rows, cells), bf16),
            pltpu.VMEM((bands, cap, cells), f32),
            pltpu.VMEM((bands, cap, cells), f32),
            pltpu.VMEM((chunks, slots + 1, rows, cells), f32),
            pltpu.VMEM((slots + 8, cells), f32),
            pltpu.VMEM((chunks, tiles, rows, cells), bf16),
            pltpu.VMEM((chunks, tiles, rows, cells), bf16),
            pltpu.VMEM((tiles, cells), f32),
            pltpu.VMEM((tiles, cells), f32),
            pltpu.VMEM((2, rows, tiles * cells), f32),
            dma((chunks, bands)),
            dma((chunks, bands)),
            dma((bands,)),
            dma((bands,)),
            dma((chunks + 1,)),
            dma((chunks + 1,)),
            dma((2,)),
        ],
        compiler_params=pltpu.CompilerParams(
            collective_id=0, has_side_effects=True, vmem_limit_bytes=60 * 1024 * 1024
        ),
        name="exchange",
    )(src, prev, last, partial, covered, wet)


def per_device(land_values, area_weights, land_mask, dest_band, dest_tile, ocean_mask):
    blocks_here = area_weights.shape[0]
    tile_cells = area_weights.shape[2]
    bands = lax.axis_size("band")
    halves = lax.axis_size("sub")
    half = lax.axis_index("sub")
    cap = max(2, 2 * blocks_here // bands)
    slots = bands * cap
    tiles = ocean_mask.shape[0] // tile_cells

    target = dest_band[:, 0]
    order = jnp.arange(blocks_here, dtype=jnp.int32)
    earlier = (target[:, None] == target[None, :]) & (order[None, :] < order[:, None])
    slot_of = target * cap + jnp.sum(earlier.astype(jnp.int32), axis=1)
    slot_ids = jnp.arange(slots, dtype=jnp.int32)
    packing = (slot_ids[:, None] == slot_of[None, :]).astype(jnp.int32)
    src = jnp.sum(packing * order[None, :], axis=1)
    tile_sent = jnp.sum(packing * (dest_tile + 1)[None, :], axis=1) - 1
    tile_sent = jnp.pad(
        tile_sent.reshape(bands, 1, cap), ((0, 0), (0, 0), (0, LANES - cap)), constant_values=-1
    )

    partial, covered, tile_recv = block_products(
        bands, land_values, area_weights, land_mask[None, :], tile_sent
    )
    tile_recv = tile_recv[:, 0, :cap].reshape(slots)

    same = (tile_recv[:, None] == tile_recv[None, :]) & (slot_ids[None, :] < slot_ids[:, None])
    prev = jnp.max(jnp.where(same, slot_ids[None, :], -1), axis=1)
    prev = jnp.where(prev < 0, slots, prev)
    listed = jnp.arange(halves * tiles, dtype=jnp.int32)
    listed = lax.rem(listed + (1 - half) * tiles, halves * tiles)
    hit = listed[:, None] == tile_recv[None, :]
    last = jnp.max(jnp.where(hit, slot_ids[None, :], -1), axis=1)
    last = jnp.where(last < 0, slots, last)

    wet = ocean_mask.reshape(tiles, tile_cells)
    return exchange(bands, cap, src, prev, last, partial, covered, wet)


def solution(mesh):
    in_specs = (
        P(None, ("band", "sub")),
        P(("band", "sub"), None, None),
        P(("band", "sub")),
        P(("band", "sub"), None),
        P(("band", "sub")),
        P(("band", "sub")),
    )
    out_specs = P(None, ("band", "sub"))
    return jax.shard_map(
        per_device, mesh=mesh, in_specs=in_specs, out_specs=out_specs, check_vma=False
    )
```

profile of v0, /device:TPU:17, one launch (start us, length us, event | category | flops | bytes accessed | tf_op | source)
XLA Modules:
  0.0 151.0 jit_solution(7864735664333541275)
XLA Ops:
  0.0 0.9 convert_reduce_fusion
  0.9 0.7 multiply_add_fusion
  1.6 0.7 select_reduce_fusion.2
  2.3 0.1 sub.10
  2.4 0.6 pad.4.t_ref
  3.0 10.9 %block_products.1 = (bf16[8,128,8,128]{3,2,1,0:T(8,128)(2,1)}, f32[128,128]{1,0:T(8,128)}, s32[16,1,128]{2,1,0:T(1,128)}) custom-call(bf16[64,16384]{1,0:T(8,128)(2,1)} %v_ref.1, bf16[128,128,128]{2,1,0:T(8,128)(2,1)} %w_ref.1, s32[1,16384]{1,0:T(1,128)} %bitcast.5, s32[16,1,128]{2,1,0:T(1,128)} %pad.4.t_ref), custom_call_target="tpu_custom_call" | custom-call | tf_op jit(solution)/shard_map/block_products/pallas_call | solution.py:88
  14.0 0.7 slice_reduce_fusion
  14.7 0.1 eq.60
  14.8 0.2 select_reduce_fusion
  15.0 0.2 select_reduce_fusion.1
  15.2 0.6 compare_select_fusion.1.prev_ref
  15.8 0.6 compare_select_fusion.last_ref
  16.3 128.6 %exchange.1 = f32[64,25600]{1,0:T(8,128)} custom-call(s32[256]{0:T(256)} %get-tuple-element.12.src_ref, s32[256]{0:T(256)} %compare_select_fusion.1.prev_ref, s32[400]{0:T(512)} %compare_select_fusion.last_ref, bf16[8,128,8,128]{3,2,1,0:T(8,128)(2,1)} %get-tuple-element.9.p_ref, f32[128,128]{1,0:T(8,128)} %get-tuple-element.10.c_ref, s32[200,128]{1,0:T(8,128)} %bitcast.4), custom_call_target="tpu_custom_call" | custom-call | tf_op jit(solution)/shard_map/exchange/pallas_call | solution.py:292
  144.9 6.1 %copy.8 = f32[64,25600]{1,0:T(8,128)} copy(f32[64,25600]{1,0:T(8,128)} %exchange.1) | data formatting | bytes 13107200
  (2 shorter events, 0.0 us)
where the time goes:
time: 151 us
  Pallas kernels  139 us (92%)
  local copies, waits for them, and re-layouts  7.62 us (5%)
  other arithmetic  3.91 us (3%)
    pallas_call x1, Pallas kernels, exchange(): pl.pallas_call(functools.partial(exchange_kernel, bands, cap, chunks, til...  129 us
    pallas_call x1, Pallas kernels, block_products(): pl.pallas_call(functools.partial(block_kernel, group, chunks, bands), gri...  10.9 us
    unnamed x1, local copies, waits for them, and re-layouts  6.12 us

commit v1 on v0

v1 whole, which is shorter than its diff:
```python
import functools

import jax
import jax.numpy as jnp
from jax import lax
from jax.experimental import pallas as pl
from jax.experimental.pallas import tpu as pltpu
from jax.sharding import PartitionSpec as P

cover_floor = 0.5
ROWS = 8
MESH = pl.DeviceIdType.MESH
f32, bf16, i32 = jnp.float32, jnp.bfloat16, jnp.int32


def target_of(me, k, size):
    peer, bit = 0, 1
    while bit < size:
        peer = peer + bit * lax.rem(me // bit + k // bit, 2)
        bit *= 2
    return peer


def block_kernel(
    group, chunks, bands, halves, v_ref, w_ref, m_ref, t_ref, p_ref, c_ref, r_ref,
    landed, send_sem, recv_sem,
):
    band = lax.axis_index("band")
    half = lax.axis_index("sub")
    cells = w_ref.shape[1]
    everyone = bands * halves

    def peer(k):
        return {
            "band": target_of(band, k // halves, bands),
            "sub": target_of(half, lax.rem(k, halves), halves),
        }

    def index_copy(k):
        return pltpu.make_async_remote_copy(
            src_ref=t_ref, dst_ref=landed.at[k],
            send_sem=send_sem.at[k], recv_sem=recv_sem.at[k],
            device_id=peer(k), device_id_type=MESH,
        )

    @pl.when(pl.program_id(0) == 0)
    def _():
        barrier = pltpu.get_barrier_semaphore()

        @pl.loop(1, everyone)
        def _(k):
            pl.semaphore_signal(barrier, inc=1, device_id=peer(k), device_id_type=MESH)

        pl.semaphore_wait(barrier, everyone - 1)

        @pl.loop(1, everyone)
        def _(k):
            index_copy(k).start()

    for j in range(group):
        lanes = pl.ds(j * cells, cells)
        mb = m_ref[:, lanes].astype(f32).astype(bf16)
        lhs = jnp.concatenate(
            [v_ref[:, lanes] * mb, jnp.broadcast_to(mb, (16, cells))], axis=0
        )
        p = jnp.dot(lhs, w_ref[j], preferred_element_type=f32)
        for c in range(chunks):
            p_ref[c, j] = p[c * ROWS:(c + 1) * ROWS].astype(bf16)
        c_ref[pl.ds(j, 1), :] = p[chunks * ROWS:chunks * ROWS + 1].astype(bf16).astype(f32)

    @pl.when(pl.program_id(0) == pl.num_programs(0) - 1)
    def _():
        @pl.loop(1, everyone)
        def _(k):
            index_copy(k).wait_send()
            index_copy(k).wait_recv()

        r_ref[0] = t_ref[...]
        r_ref[pl.ds(1, everyone - 1)] = landed[pl.ds(1, everyone - 1)]


def block_products(bands, halves, values, weights, mask, owners):
    fields = values.shape[0]
    blocks, cells, out_cells = weights.shape
    chunks = fields // ROWS
    group = 16
    everyone = bands * halves
    return pl.pallas_call(
        functools.partial(block_kernel, group, chunks, bands, halves),
        grid=(blocks // group,),
        in_specs=[
            pl.BlockSpec((fields, group * cells), lambda i: (0, i)),
            pl.BlockSpec((group, cells, out_cells), lambda i: (i, 0, 0)),
            pl.BlockSpec((1, group * cells), lambda i: (0, i)),
            pl.BlockSpec(memory_space=pltpu.VMEM),
        ],
        out_specs=[
            pl.BlockSpec((chunks, group, ROWS, out_cells), lambda i: (0, i, 0, 0)),
            pl.BlockSpec((group, out_cells), lambda i: (i, 0)),
            pl.BlockSpec(memory_space=pltpu.VMEM),
        ],
        out_shape=[
            jax.ShapeDtypeStruct((chunks, blocks, ROWS, out_cells), bf16),
            jax.ShapeDtypeStruct((blocks, out_cells), f32),
            jax.ShapeDtypeStruct((everyone, 1, blocks), i32),
        ],
        scratch_shapes=[
            pltpu.VMEM((everyone, 1, blocks), i32),
            pltpu.SemaphoreType.DMA((everyone,)),
            pltpu.SemaphoreType.DMA((everyone,)),
        ],
        compiler_params=pltpu.CompilerParams(collective_id=1, has_side_effects=True),
        name="block_products",
    )(values, weights, mask, owners)


def exchange_kernel(
    shape, src1_ref, src2_ref, p_ref, c_ref, out_ref, cout_ref, *scratch
):
    bands, halves, planes, own, first, second, chunks = shape
    wide = bands // planes
    inside = wide * halves
    send1, send2, csend1, crecv1, cheld, csend2, cstage = scratch[:7]
    sem1, rem1, sem2, rem2, csem1, crem1, csem2, crem2, lsem, clsem = scratch[7:17]
    recv1 = scratch[17:]
    band = lax.axis_index("band")
    half = lax.axis_index("sub")

    def z_peer(k):
        return {"band": target_of(band, k * wide, bands)}

    def plane_peer(k):
        return {
            "band": target_of(band, k // halves, bands),
            "sub": target_of(half, lax.rem(k, halves), halves),
        }

    barrier = pltpu.get_barrier_semaphore()

    @pl.loop(1, planes)
    def _(k):
        pl.semaphore_signal(barrier, inc=1, device_id=z_peer(k), device_id_type=MESH)

    @pl.loop(1, inside)
    def _(k):
        pl.semaphore_signal(barrier, inc=1, device_id=plane_peer(k), device_id_type=MESH)

    pl.semaphore_wait(barrier, planes + inside - 2)

    def z_copy(c, k):
        return pltpu.make_async_remote_copy(
            src_ref=send1.at[c, k],
            dst_ref=recv1[c].at[pl.ds(own + (k - 1) * first, first)],
            send_sem=sem1.at[c, k], recv_sem=rem1.at[c, k],
            device_id=z_peer(k), device_id_type=MESH,
        )

    def plane_copy(c, k):
        return pltpu.make_async_remote_copy(
            src_ref=send2.at[c, k], dst_ref=out_ref.at[c, k],
            send_sem=sem2.at[c, k], recv_sem=rem2.at[c, k],
            device_id=plane_peer(k), device_id_type=MESH,
        )

    def z_cover(k):
        return pltpu.make_async_remote_copy(
            src_ref=csend1.at[k], dst_ref=crecv1.at[k],
            send_sem=csem1.at[k], recv_sem=crem1.at[k],
            device_id=z_peer(k), device_id_type=MESH,
        )

    def plane_cover(k):
        return pltpu.make_async_remote_copy(
            src_ref=csend2.at[k], dst_ref=cout_ref.at[k],
            send_sem=csem2.at[k], recv_sem=crem2.at[k],
            device_id=plane_peer(k), device_id_type=MESH,
        )

    def local_copy(c):
        return pltpu.make_async_copy(send2.at[c, 0], out_ref.at[c, 0], lsem.at[c])

    local_cover = pltpu.make_async_copy(csend2.at[0], cout_ref.at[0], clsem)

    def send_chunk(c):
        @pl.loop(1, planes)
        def _(k):
            for j in range(first):
                send1[c, k, j] = p_ref[c, src1_ref[own + (k - 1) * first + j]]
            z_copy(c, k).start()

        for j in range(own):
            recv1[c][j] = p_ref[c, src1_ref[j]]

    def forward_chunk(c):
        @pl.loop(1, planes)
        def _(k):
            z_copy(c, k).wait_recv()

        @pl.loop(1, inside)
        def _(k):
            for j in range(second):
                send2[c, k, j] = recv1[c][src2_ref[k * second + j]]
            plane_copy(c, k).start()

        for j in range(second):
            send2[c, 0, j] = recv1[c][src2_ref[j]]
        local_copy(c).start()

    send_chunk(0)

    @pl.loop(1, planes)
    def _(k):
        for j in range(first):
            cstage[pl.ds(j, 1), :] = c_ref[pl.ds(src1_ref[own + (k - 1) * first + j], 1), :]
        csend1[k] = cstage[pl.ds(0, first), :].astype(bf16)
        z_cover(k).start()

    for j in range(own):
        cheld[pl.ds(j, 1), :] = c_ref[pl.ds(src1_ref[j], 1), :]

    for c in range(1, chunks):
        send_chunk(c)

    for c in range(chunks):
        forward_chunk(c)
        if c == 0:
            for k in range(1, planes):
                z_cover(k).wait_recv()
                cheld[pl.ds(own + (k - 1) * first, first), :] = crecv1[k].astype(f32)

            @pl.loop(0, inside)
            def _(k):
                for j in range(second):
                    cstage[pl.ds(j, 1), :] = cheld[pl.ds(src2_ref[k * second + j], 1), :]
                csend2[k] = cstage[pl.ds(0, second), :].astype(bf16)

            @pl.loop(1, inside)
            def _(k):
                plane_cover(k).start()

            local_cover.start()

    @pl.loop(1, inside)
    def _(k):
        plane_cover(k).wait_recv()
        for c in range(chunks):
            plane_copy(c, k).wait_recv()

    local_cover.wait()
    for c in range(chunks):
        local_copy(c).wait()

    @pl.loop(1, planes)
    def _(k):
        z_cover(k).wait_send()
        for c in range(chunks):
            z_copy(c, k).wait_send()

    @pl.loop(1, inside)
    def _(k):
        plane_cover(k).wait_send()
        for c in range(chunks):
            plane_copy(c, k).wait_send()


def exchange(shape, ident, src1, src2, partial, covered):
    bands, halves, planes, own, first, second, chunks = shape
    _, _, rows, cells = partial.shape
    inside = bands * halves // planes
    held = own + (planes - 1) * first
    smem = pl.BlockSpec(memory_space=pltpu.SMEM)
    vmem = pl.BlockSpec(memory_space=pltpu.VMEM)
    hbm = pl.BlockSpec(memory_space=pl.ANY)
    dma = pltpu.SemaphoreType.DMA
    return pl.pallas_call(
        functools.partial(exchange_kernel, shape),
        in_specs=[smem, smem, vmem, vmem],
        out_specs=[hbm, hbm],
        out_shape=[
            jax.ShapeDtypeStruct((chunks, inside, second, rows, cells), bf16),
            jax.ShapeDtypeStruct((inside, second, cells), bf16),
        ],
        scratch_shapes=[
            pltpu.VMEM((chunks, planes, first, rows, cells), bf16),
            pltpu.VMEM((chunks, inside, second, rows, cells), bf16),
            pltpu.VMEM((planes, first, cells), bf16),
            pltpu.VMEM((planes, first, cells), bf16),
            pltpu.VMEM((held, cells), f32),
            pltpu.VMEM((inside, second, cells), bf16),
            pltpu.VMEM((max(first, second), cells), f32),
            dma((chunks, planes)),
            dma((chunks, planes)),
            dma((chunks, inside)),
            dma((chunks, inside)),
            dma((planes,)),
            dma((planes,)),
            dma((inside,)),
            dma((inside,)),
            dma((chunks,)),
            dma,
        ] + [pltpu.VMEM((held, rows, cells), bf16) for _ in range(chunks)],
        compiler_params=pltpu.CompilerParams(
            collective_id=ident, has_side_effects=True, vmem_limit_bytes=60 * 1024 * 1024
        ),
        name="exchange",
    )(src1, src2, partial, covered)


def gather_kernel(chunks, tiles, slot_ref, r_ref, c_ref, wet_ref, out_ref, acc, cacc, done, sem):
    step = pl.program_id(0)
    second = r_ref.shape[2]
    cells = r_ref.shape[4]
    unroll = 8

    @pl.when(step == 0)
    def _():
        @pl.loop(0, tiles)
        def _(t):
            for c in range(chunks):
                acc[c, t] = jnp.zeros((ROWS, cells), f32)

        cacc[...] = jnp.zeros_like(cacc)

    @pl.loop(0, second // unroll)
    def _(g):
        cov = c_ref[0, pl.ds(pl.multiple_of(g * unroll, unroll), unroll), :].astype(f32)
        for u in range(unroll):
            j = g * unroll + u
            t = slot_ref[step * second + j]
            for c in range(chunks):
                acc[c, t] += r_ref[c, 0, j].astype(f32)
            cacc[pl.ds(t, 1), :] += cov[u:u + 1]

    @pl.when(step == pl.num_programs(0) - 1)
    def _():
        cacc[pl.ds(0, tiles), :] = wet_ref[...].astype(f32) / jnp.maximum(
            cacc[pl.ds(0, tiles), :], cover_floor
        )

        def out_copy(c):
            return pltpu.make_async_copy(
                done.at[c], out_ref.at[pl.ds(c * ROWS, ROWS), :], sem.at[c]
            )

        for c in range(chunks):
            @pl.loop(0, tiles // unroll)
            def _(g, c=c):
                for u in range(unroll):
                    t = g * unroll + u
                    lanes = pl.ds(pl.multiple_of(t * cells, cells), cells)
                    done[c, :, lanes] = acc[c, t] * cacc[pl.ds(t, 1), :]

            out_copy(c).start()

        for c in range(chunks):
            out_copy(c).wait()


def gather(slots, arrived, covers, wet):
    chunks, inside, second, rows, cells = arrived.shape
    tiles = wet.shape[0]
    return pl.pallas_call(
        functools.partial(gather_kernel, chunks, tiles),
        grid=(inside,),
        in_specs=[
            pl.BlockSpec(memory_space=pltpu.SMEM),
            pl.BlockSpec((chunks, 1, second, rows, cells), lambda i: (0, i, 0, 0, 0)),
            pl.BlockSpec((1, second, cells), lambda i: (i, 0, 0)),
            pl.BlockSpec((tiles, cells), lambda i: (0, 0)),
        ],
        out_specs=pl.BlockSpec(memory_space=pl.ANY),
        out_shape=jax.ShapeDtypeStruct((chunks * rows, tiles * cells), f32),
        scratch_shapes=[
            pltpu.VMEM((chunks, tiles + 1, rows, cells), f32),
            pltpu.VMEM((tiles + 8, cells), f32),
            pltpu.VMEM((chunks, rows, tiles * cells), f32),
            pltpu.SemaphoreType.DMA((chunks,)),
        ],
        compiler_params=pltpu.CompilerParams(vmem_limit_bytes=60 * 1024 * 1024),
        name="gather",
    )(slots, arrived, covers, wet)


def earlier(masks):
    size = masks.shape[1]
    order = jnp.arange(size, dtype=i32)
    before = (order[:, None] < order[None, :]).astype(bf16)
    return jnp.dot(masks.astype(bf16), before, preferred_element_type=f32).astype(i32)


def pick(masks, rank, room, values):
    slot = jnp.arange(room, dtype=i32)
    hit = masks[:, None, :] & (rank[:, None, :] == slot[None, :, None])
    return jnp.sum(jnp.where(hit, values, 0), axis=2)


def per_device(land_values, area_weights, land_mask, dest_band, dest_tile, ocean_mask):
    blocks = area_weights.shape[0]
    cells = area_weights.shape[2]
    chunks = land_values.shape[0] // ROWS
    bands = lax.axis_size("band")
    halves = lax.axis_size("sub")
    everyone = bands * halves
    me = lax.axis_index("band") * halves + lax.axis_index("sub")
    tiles = ocean_mask.shape[0] // cells
    cap = max(2, 2 * blocks // bands)
    planes = 2 ** ((bands.bit_length() - 1) // 2)
    wide = bands // planes
    inside = wide * halves
    shift = (tiles - 1).bit_length()

    tile = dest_band[:, 0] * (halves * tiles) + dest_tile
    owner = tile // tiles
    packed = owner * (1 << shift) + (tile - owner * tiles)

    partial, covered, landed = block_products(
        bands, halves, land_values, area_weights, land_mask[None, :], packed[None, :]
    )

    landed = landed.reshape(planes, inside, blocks)
    rel = (landed >> shift) ^ me
    local = landed & ((1 << shift) - 1)
    queue = planes * blocks

    rel_mine = rel[0, 0]
    mine = (rel_mine // inside)[None, :] == jnp.arange(planes, dtype=i32)[:, None]
    mine = jnp.pad(mine, ((0, 0), (0, queue - blocks)))
    column = rel[:, 0, :].reshape(1, queue)
    here = column < inside
    row_of = jnp.arange(queue, dtype=i32)[None, :] // blocks
    per_row = here & (row_of == jnp.arange(planes, dtype=i32)[:, None])
    to_dest = column == jnp.arange(inside, dtype=i32)[:, None]
    to_me = (rel == 0).transpose(1, 0, 2).reshape(inside, queue)
    local_of = local.transpose(1, 0, 2).reshape(inside, queue)
    ranks = earlier(jnp.concatenate([mine, per_row, to_dest, to_me], axis=0))
    rank_mine, rank_row, rank_dest, rank_me = jnp.split(
        ranks, [planes, 2 * planes, 2 * planes + inside]
    )
    rank_row = jnp.sum(jnp.where(per_row, rank_row, 0), axis=0, keepdims=True)

    source = jnp.arange(everyone, dtype=i32).reshape(planes, inside, 1)
    plane_of = (rel ^ source) // inside
    load1 = jnp.max(jnp.stack(
        [jnp.sum((plane_of == k).astype(i32), axis=2) for k in range(1, planes)]
    ))
    by_column = rel.transpose(1, 0, 2).reshape(inside, 1, queue)
    load2 = jnp.max(jnp.sum(
        (by_column == jnp.arange(everyone, dtype=i32)[None, :, None]).astype(i32), axis=2
    ))

    wet = ocean_mask.reshape(tiles, cells)
    own = min(blocks, wide * cap)
    most = min(queue, planes * cap)
    mean1 = blocks // planes
    mean2 = max(1, queue // everyone)
    rooms = [
        (min(own, 3 * mean1 // 2), min(most, 3 * mean2)),
        (min(own, 7 * mean1 // 4), min(most, 3 * mean2)),
        (own, most),
    ]

    def run(ident, first, second):
        src1 = jnp.concatenate([
            pick(mine[:1, :blocks], rank_mine[:1, :blocks], own, jnp.arange(blocks, dtype=i32))[0],
            pick(
                mine[1:, :blocks], rank_mine[1:, :blocks], first, jnp.arange(blocks, dtype=i32)
            ).reshape(-1),
        ])
        base = jnp.where(row_of == 0, 0, own + (row_of - 1) * first)
        src2 = pick(to_dest, rank_dest, second, base + rank_row).reshape(-1)
        slots = pick(to_me, rank_me, second, (local_of - tiles)[:, None, :]).reshape(-1) + tiles
        shape = (bands, halves, planes, own, first, second, chunks)
        arrived, covers = exchange(shape, ident, src1, src2, partial, covered)
        return gather(slots, arrived, covers, wet)

    fits = [(load1 <= first) & (load2 <= second) for first, second in rooms[:-1]]
    choice = len(rooms) - 1
    for n in reversed(range(len(fits))):
        choice = jnp.where(fits[n], n, choice)
    return lax.switch(
        choice, [lambda n=n: run(2 + n, *rooms[n]) for n in range(len(rooms))]
    )


def solution(mesh):
    in_specs = (
        P(None, ("band", "sub")),
        P(("band", "sub"), None, None),
        P(("band", "sub")),
        P(("band", "sub"), None),
        P(("band", "sub")),
        P(("band", "sub")),
    )
    out_specs = P(None, ("band", "sub"))
    return jax.shard_map(
        per_device, mesh=mesh, in_specs=in_specs, out_specs=out_specs, check_vma=False
    )
```

time: 151 us -> 137 us (0.907)
  Pallas kernels: 139 us -> 123 us
  local copies, waits for them, and re-layouts: 7.62 us -> 1.52 us
  other arithmetic: 3.91 us -> 8.26 us
  between operations: 0.03 us -> 2.95 us
    pallas_call x2 -> x3, Pallas kernels: 139 us -> 123 us  [the longest x1 99.2 us: exchange(): pl.pallas_call(functools.partial(exchange_kernel, shape), in_specs=[smem,...]
    unnamed x1 -> x2, local copies, waits for them, and re-layouts: 6.12 us -> 0.01 us
    reduce_max x2 -> x4, other arithmetic: 0.42 us -> 2.62 us  [the longest x3 1.99 us: per_device(): jnp.max(jnp.stack([jnp.sum((plane_of == k).astype(i32), axis=2) for k in...]
where the time goes in v1:
time: 137 us; the launch traced here: 136 us
  Pallas kernels  123 us (90%)
  other arithmetic  8.26 us (6%)
  between operations  2.95 us (2%)
  local copies, waits for them, and re-layouts  1.52 us (1%)
    pallas_call x1, Pallas kernels, exchange(): pl.pallas_call(functools.partial(exchange_kernel, shape), in_specs=[smem,...  99.2 us
    pallas_call x1, Pallas kernels, block_products(): pl.pallas_call(functools.partial(block_kernel, group, chunks, bands, halv...  12.1 us
    pallas_call x1, Pallas kernels, gather(): pl.pallas_call(functools.partial(gather_kernel, chunks, tiles), grid=(ins...  11.6 us

profile of v1, /device:TPU:17, one launch (start us, length us, event | category | flops | bytes accessed | tf_op | source)
XLA Modules:
  0.0 136.1 jit_solution(2154010689030383249)
XLA Ops:
  0.0 0.0 copy-start
  0.0 1.2 add_bitcast_fusion.3.t_ref
  1.2 0.1 reshape.437
  1.3 12.1 %block_products.1 = (bf16[8,128,8,128]{3,2,1,0:T(8,128)(2,1)S(1)}, f32[128,128]{1,0:T(8,128)S(1)}, s32[32,1,128]{2,1,0:T(1,128)}) custom-call(bf16[64,16384]{1,0:T(8,128)(2,1)} %v_ref.1, bf16[128,128,128]{2,1,0:T(8,128)(2,1)} %w_ref.1, s32[1,16384]{1,0:T(1,128)} %bitcast.73, s32[1,128]{1,0:T(1,128)} %add_bitcast_fusion.3.t_ref), custom_call_target="tpu_custom_call" | custom-call | tf_op jit(solution)/shard_map/block_products/pallas_call | solution.py:88
  13.5 0.9 and_select_fusion
  14.4 1.8 %fusion.30 = (s32[32]{0:T(128)S(1)}, s32[32]{0:T(128)S(1)}, s32[32]{0:T(128)S(1)}) fusion(s32[32,1,128]{2,1,0:T(1,128)S(1)} %get-tuple-element.232), kind=kLoop, calls=%fused_computation.89 | loop fusion | flops 36768 | bytes 16768 | tf_op jit(solution)/shard_map/reduce_sum | solution.py:444
  16.2 0.6 reduce_max.25
  16.8 0.7 reduce_max.29
  18.9 0.6 reduce_max.37
  20.3 0.2 convert_reduce_fusion
  20.5 0.6 reduce_max.39
  21.8 0.2 convolution_convert_fusion
  22.0 0.0 copy-done
  22.0 113.9 %conditional.1 = (f32[64,25600]{1,0:T(8,128)}) conditional(s32[]{:T(128)} %clamp.3, (pred[8,4,128]{2,0,1:T(8,128)(4,1)S(1)}, s32[24,512]{1,0:T(8,128)S(1)}, s32[8,4,128]{2,0,1:T(8,128)S(1)}, pred[4,512]{1,0:T(4,128)(4,1)S(1)}, s32[24,512]{1,0:T(8,128)S(1)}, /*index=5*/pred[8,512]{1,0:T(8,128)(4,1)S(1)}, ...), branch_computations={%region_9.14_spmd, %region_14.19_spmd, %region_19.24_spmd} | conditional | flops 2242048 | bytes 210976 | solution.py:480
  22.0 0.1 select_reduce_fusion.3
  22.2 0.1 select_reduce_fusion.2
  22.4 0.1 reshape.421
  22.5 0.6 pad_add_fusion.src1_ref
  23.1 0.3 select_reduce_fusion.1
  23.4 0.7 add.64.slot_ref
  24.0 0.3 select_reduce_fusion
  24.3 0.7 reshape.422.src2_ref
  24.9 99.2 %exchange.3 = (bf16[8,8,48,8,128]{4,3,2,1,0:T(8,128)(2,1)}, bf16[8,48,128]{2,1,0:T(8,128)(2,1)}) custom-call(s32[208]{0:T(256)} %pad_add_fusion.src1_ref, s32[384]{0:T(512)} %reshape.422.src2_ref, bf16[8,128,8,128]{3,2,1,0:T(8,128)(2,1)S(1)} %get-tuple-element.90.p_ref, f32[128,128]{1,0:T(8,128)S(1)} %get-tuple-element.91.c_ref), custom_call_target="tpu_custom_call" | custom-call | tf_op jit(solution)/shard_map/cond/branch_0_fun/exchange/pallas_call | solution.py:275
  124.1 11.6 %gather.3 = f32[64,25600]{1,0:T(8,128)} custom-call(s32[384]{0:T(512)} %add.64.slot_ref, bf16[8,8,48,8,128]{4,3,2,1,0:T(8,128)(2,1)} %get-tuple-element.92.r_ref, bf16[8,48,128]{2,1,0:T(8,128)(2,1)} %get-tuple-element.93.c_ref, s32[200,128]{1,0:T(8,128)S(1)} %bitcast.62), custom_call_target="tpu_custom_call" | custom-call | tf_op jit(solution)/shard_map/cond/branch_0_fun/gather/pallas_call | solution.py:362
  (23 shorter events, 0.2 us)
Async XLA Ops:
  0.0 22.0 %copy-start = (s32[25600]{0:T(1024)S(1)}, s32[25600]{0:T(1024)}, u32[]{:S(2)}) copy-start(s32[25600]{0:T(1024)} %param.14) | copy-start | bytes 307204

commit v2 on v1

v2 whole, which is shorter than its diff:
```python
import functools

import jax
import jax.numpy as jnp
from jax import lax
from jax.experimental import pallas as pl
from jax.experimental.pallas import tpu as pltpu
from jax.sharding import PartitionSpec as P

cover_floor = 0.5
ROWS = 8
MESH = pl.DeviceIdType.MESH
f32, bf16, i32 = jnp.float32, jnp.bfloat16, jnp.int32


def target_of(me, k, size):
    peer, bit = 0, 1
    while bit < size:
        peer = peer + bit * lax.rem(me // bit + k // bit, 2)
        bit *= 2
    return peer


def block_kernel(
    group, chunks, bands, halves, v_ref, w_ref, m_ref, t_ref, p_ref, c_ref, r_ref,
    landed, send_sem, recv_sem,
):
    band = lax.axis_index("band")
    half = lax.axis_index("sub")
    cells = w_ref.shape[1]
    everyone = bands * halves

    def peer(k):
        return {
            "band": target_of(band, k // halves, bands),
            "sub": target_of(half, lax.rem(k, halves), halves),
        }

    def index_copy(k):
        return pltpu.make_async_remote_copy(
            src_ref=t_ref, dst_ref=landed.at[k],
            send_sem=send_sem.at[k], recv_sem=recv_sem.at[k],
            device_id=peer(k), device_id_type=MESH,
        )

    @pl.when(pl.program_id(0) == 0)
    def _():
        barrier = pltpu.get_barrier_semaphore()

        @pl.loop(1, everyone)
        def _(k):
            pl.semaphore_signal(barrier, inc=1, device_id=peer(k), device_id_type=MESH)

        pl.semaphore_wait(barrier, everyone - 1)

        @pl.loop(1, everyone)
        def _(k):
            index_copy(k).start()

    for j in range(group):
        lanes = pl.ds(j * cells, cells)
        mb = m_ref[:, lanes].astype(f32).astype(bf16)
        lhs = jnp.concatenate(
            [v_ref[:, lanes] * mb, jnp.broadcast_to(mb, (16, cells))], axis=0
        )
        p = jnp.dot(lhs, w_ref[j], preferred_element_type=f32)
        for c in range(chunks):
            p_ref[c, j] = p[c * ROWS:(c + 1) * ROWS].astype(bf16)
        c_ref[pl.ds(j, 1), :] = p[chunks * ROWS:chunks * ROWS + 1].astype(bf16).astype(f32)

    @pl.when(pl.program_id(0) == pl.num_programs(0) - 1)
    def _():
        @pl.loop(1, everyone)
        def _(k):
            index_copy(k).wait_send()
            index_copy(k).wait_recv()

        r_ref[0] = t_ref[...]
        r_ref[pl.ds(1, everyone - 1)] = landed[pl.ds(1, everyone - 1)]


def block_products(bands, halves, values, weights, mask, owners):
    fields = values.shape[0]
    blocks, cells, out_cells = weights.shape
    chunks = fields // ROWS
    group = 16
    everyone = bands * halves
    return pl.pallas_call(
        functools.partial(block_kernel, group, chunks, bands, halves),
        grid=(blocks // group,),
        in_specs=[
            pl.BlockSpec((fields, group * cells), lambda i: (0, i)),
            pl.BlockSpec((group, cells, out_cells), lambda i: (i, 0, 0)),
            pl.BlockSpec((1, group * cells), lambda i: (0, i)),
            pl.BlockSpec(memory_space=pltpu.VMEM),
        ],
        out_specs=[
            pl.BlockSpec((chunks, group, ROWS, out_cells), lambda i: (0, i, 0, 0)),
            pl.BlockSpec((group, out_cells), lambda i: (i, 0)),
            pl.BlockSpec(memory_space=pltpu.VMEM),
        ],
        out_shape=[
            jax.ShapeDtypeStruct((chunks, blocks, ROWS, out_cells), bf16),
            jax.ShapeDtypeStruct((blocks, out_cells), f32),
            jax.ShapeDtypeStruct((everyone, 1, blocks), i32),
        ],
        scratch_shapes=[
            pltpu.VMEM((everyone, 1, blocks), i32),
            pltpu.SemaphoreType.DMA((everyone,)),
            pltpu.SemaphoreType.DMA((everyone,)),
        ],
        compiler_params=pltpu.CompilerParams(collective_id=1, has_side_effects=True),
        name="block_products",
    )(values, weights, mask, owners)


def exchange_kernel(
    shape, list_ref, p_ref, c_ref, wet_ref, out_ref, *scratch
):
    bands, halves, planes, room1, room2, first, second, chunks, tiles = shape
    wide = bands // planes
    inside = wide * halves
    cover1, cover2 = -(-first // 8) * 8, -(-second // 8) * 8
    slots = inside * room2
    send1, send2, recv2, run, done = scratch[:5]
    csend1, crecv1, cheld, csend2, crecv2, cstage, crun, factor = scratch[5:13]
    sem1, rem1, sem2, rem2, csem1, crem1, csem2, crem2, out_sem = scratch[13:22]
    recv1 = scratch[22:]
    band = lax.axis_index("band")
    half = lax.axis_index("sub")
    cells = c_ref.shape[1]
    at2 = planes * room1
    at_prev = at2 + slots
    at_last = at_prev + slots

    def z_peer(k):
        return {"band": target_of(band, k * wide, bands)}

    def plane_peer(k):
        return {
            "band": target_of(band, k // halves, bands),
            "sub": target_of(half, lax.rem(k, halves), halves),
        }

    barrier = pltpu.get_barrier_semaphore()

    @pl.loop(1, planes)
    def _(k):
        pl.semaphore_signal(barrier, inc=1, device_id=z_peer(k), device_id_type=MESH)

    @pl.loop(1, inside)
    def _(k):
        pl.semaphore_signal(barrier, inc=1, device_id=plane_peer(k), device_id_type=MESH)

    pl.semaphore_wait(barrier, planes + inside - 2)

    def z_copy(c, k):
        return pltpu.make_async_remote_copy(
            src_ref=send1.at[c, k],
            dst_ref=recv1[c].at[pl.ds(k * room1, first)],
            send_sem=sem1.at[c, k], recv_sem=rem1.at[c, k],
            device_id=z_peer(k), device_id_type=MESH,
        )

    def plane_copy(c, k):
        return pltpu.make_async_remote_copy(
            src_ref=send2.at[c, k], dst_ref=recv2.at[c, k],
            send_sem=sem2.at[c, k], recv_sem=rem2.at[c, k],
            device_id=plane_peer(k), device_id_type=MESH,
        )

    def z_cover(k):
        return pltpu.make_async_remote_copy(
            src_ref=csend1.at[k], dst_ref=crecv1.at[k],
            send_sem=csem1.at[k], recv_sem=crem1.at[k],
            device_id=z_peer(k), device_id_type=MESH,
        )

    def plane_cover(k):
        return pltpu.make_async_remote_copy(
            src_ref=csend2.at[k], dst_ref=crecv2.at[k],
            send_sem=csem2.at[k], recv_sem=crem2.at[k],
            device_id=plane_peer(k), device_id_type=MESH,
        )

    def out_copy(c):
        return pltpu.make_async_copy(
            done.at[c % 2], out_ref.at[pl.ds(c * ROWS, ROWS), :], out_sem.at[c % 2]
        )

    def each(count, body, step=16):
        @pl.loop(0, count // step)
        def _(g):
            for u in range(step):
                body(g * step + u)

        for j in range(count // step * step, count):
            body(j)

    def send_chunk(c):
        @pl.loop(1, planes)
        def _(k):
            def pack(j):
                send1[c, k, j] = p_ref[c, list_ref[k * room1 + j]]

            each(first, pack)
            z_copy(c, k).start()

        def keep(j):
            recv1[c][j] = p_ref[c, list_ref[j]]

        each(room1, keep)

    def forward_chunk(c):
        @pl.loop(1, inside)
        def _(k):
            def pack(j):
                send2[c, k, j] = recv1[c][list_ref[at2 + k * room2 + j]]

            each(second, pack)
            plane_copy(c, k).start()

    def add_chunk(c):
        run[slots] = jnp.zeros((ROWS, cells), f32)

        def own_slot(j):
            run[j] = run[list_ref[at_prev + j]] + recv1[c][list_ref[at2 + j]].astype(f32)

        each(second, own_slot)

        @pl.loop(1, inside)
        def _(k):
            plane_copy(c, k).wait_recv()

            def one(j):
                i = k * room2 + j
                run[i] = run[list_ref[at_prev + i]] + recv2[c, k, j].astype(f32)

            each(second, one)

        if c >= 2:
            out_copy(c - 2).wait()

        def finish(t):
            lanes = pl.ds(pl.multiple_of(t * cells, cells), cells)
            done[c % 2, :, lanes] = run[list_ref[at_last + t]] * factor[pl.ds(t, 1), :]

        each(tiles, finish)
        out_copy(c).start()

    def send_covers():
        @pl.loop(1, planes)
        def _(k):
            def pack(j):
                cstage[pl.ds(j, 1), :] = c_ref[pl.ds(list_ref[k * room1 + j], 1), :]

            each(first, pack)
            csend1[k] = cstage[pl.ds(0, cover1), :].astype(bf16)
            z_cover(k).start()

        def keep(j):
            cheld[pl.ds(j, 1), :] = c_ref[pl.ds(list_ref[j], 1), :]

        each(room1, keep)

    def forward_covers():
        for k in range(1, planes):
            z_cover(k).wait_recv()
            cheld[pl.ds(k * room1, cover1), :] = crecv1[k].astype(f32)

        @pl.loop(1, inside)
        def _(k):
            def pack(j):
                cstage[pl.ds(j, 1), :] = cheld[pl.ds(list_ref[at2 + k * room2 + j], 1), :]

            each(second, pack)
            csend2[k] = cstage[pl.ds(0, cover2), :].astype(bf16)
            plane_cover(k).start()

    def add_covers():
        crun[pl.ds(slots, 8), :] = jnp.zeros((8, cells), f32)

        def own_slot(j):
            crun[pl.ds(j, 1), :] = (
                crun[pl.ds(list_ref[at_prev + j], 1), :]
                + cheld[pl.ds(list_ref[at2 + j], 1), :]
            )

        each(second, own_slot)

        @pl.loop(1, inside)
        def _(k):
            plane_cover(k).wait_recv()
            cstage[pl.ds(0, cover2), :] = crecv2[k].astype(f32)

            def one(j):
                i = k * room2 + j
                crun[pl.ds(i, 1), :] = (
                    crun[pl.ds(list_ref[at_prev + i], 1), :] + cstage[pl.ds(j, 1), :]
                )

            each(second, one)

        def total(t):
            factor[pl.ds(t, 1), :] = crun[pl.ds(list_ref[at_last + t], 1), :]

        each(tiles, total)
        factor[...] = wet_ref[...].astype(f32) / jnp.maximum(factor[...], cover_floor)

    window, lag = 2, 2
    cstage[...] = jnp.zeros_like(cstage)
    send_chunk(0)
    send_covers()
    for c in range(1, min(window, chunks)):
        send_chunk(c)

    for c in range(chunks):
        @pl.loop(1, planes)
        def _(k, c=c):
            z_copy(c, k).wait_recv()

        if c + window < chunks:
            send_chunk(c + window)
        forward_chunk(c)
        if c == 0:
            forward_covers()
        if c == lag:
            add_covers()
        if c >= lag:
            add_chunk(c - lag)

    for c in range(chunks - lag, chunks):
        add_chunk(c)

    @pl.loop(1, planes)
    def _(k):
        z_cover(k).wait_send()
        for c in range(chunks):
            z_copy(c, k).wait_send()

    @pl.loop(1, inside)
    def _(k):
        plane_cover(k).wait_send()
        for c in range(chunks):
            plane_copy(c, k).wait_send()

    for c in range(chunks - 2, chunks):
        out_copy(c).wait()


def exchange(shape, ident, lists, partial, covered, wet):
    bands, halves, planes, room1, room2, first, second, chunks, tiles = shape
    _, _, rows, cells = partial.shape
    inside = bands * halves // planes
    slots = inside * room2
    cover1, cover2 = -(-first // 8) * 8, -(-second // 8) * 8
    smem = pl.BlockSpec(memory_space=pltpu.SMEM)
    vmem = pl.BlockSpec(memory_space=pltpu.VMEM)
    dma = pltpu.SemaphoreType.DMA
    return pl.pallas_call(
        functools.partial(exchange_kernel, shape),
        in_specs=[smem, vmem, vmem, vmem],
        out_specs=pl.BlockSpec(memory_space=pl.ANY),
        out_shape=jax.ShapeDtypeStruct((chunks * rows, tiles * cells), f32),
        scratch_shapes=[
            pltpu.VMEM((chunks, planes, first, rows, cells), bf16),
            pltpu.VMEM((chunks, inside, second, rows, cells), bf16),
            pltpu.VMEM((chunks, inside, second, rows, cells), bf16),
            pltpu.VMEM((slots + 1, rows, cells), f32),
            pltpu.VMEM((2, rows, tiles * cells), f32),
            pltpu.VMEM((planes, cover1, cells), bf16),
            pltpu.VMEM((planes, cover1, cells), bf16),
            pltpu.VMEM((planes * room1, cells), f32),
            pltpu.VMEM((inside, cover2, cells), bf16),
            pltpu.VMEM((inside, cover2, cells), bf16),
            pltpu.VMEM((max(cover1, cover2), cells), f32),
            pltpu.VMEM((slots + 8, cells), f32),
            pltpu.VMEM((tiles, cells), f32),
            dma((chunks, planes)),
            dma((chunks, planes)),
            dma((chunks, inside)),
            dma((chunks, inside)),
            dma((planes,)),
            dma((planes,)),
            dma((inside,)),
            dma((inside,)),
            dma((2,)),
        ] + [pltpu.VMEM((planes * room1, rows, cells), bf16) for _ in range(chunks)],
        compiler_params=pltpu.CompilerParams(
            collective_id=ident, has_side_effects=True, vmem_limit_bytes=40 * 1024 * 1024
        ),
        name="exchange",
    )(lists, partial, covered, wet)


def earlier(masks):
    size = masks.shape[1]
    order = jnp.arange(size, dtype=i32)
    before = (order[:, None] < order[None, :]).astype(bf16)
    return jnp.dot(masks.astype(bf16), before, preferred_element_type=f32).astype(i32)


def pick(masks, rank, room, values):
    slot = jnp.arange(room, dtype=i32)
    hit = masks[:, None, :] & (rank[:, None, :] == slot[None, :, None])
    return jnp.sum(jnp.where(hit, values, 0), axis=2)


def per_device(land_values, area_weights, land_mask, dest_band, dest_tile, ocean_mask):
    blocks = area_weights.shape[0]
    cells = area_weights.shape[2]
    chunks = land_values.shape[0] // ROWS
    bands = lax.axis_size("band")
    halves = lax.axis_size("sub")
    everyone = bands * halves
    me = lax.axis_index("band") * halves + lax.axis_index("sub")
    tiles = ocean_mask.shape[0] // cells
    cap = max(2, 2 * blocks // bands)
    planes = 2 ** ((bands.bit_length() - 1) // 2)
    wide = bands // planes
    inside = wide * halves
    shift = (tiles - 1).bit_length()

    tile = dest_band[:, 0] * (halves * tiles) + dest_tile
    owner = tile // tiles
    packed = owner * (1 << shift) + (tile - owner * tiles)

    partial, covered, landed = block_products(
        bands, halves, land_values, area_weights, land_mask[None, :], packed[None, :]
    )

    landed = landed.reshape(planes, inside, blocks)
    rel = (landed >> shift) ^ me
    local = landed & ((1 << shift) - 1)
    queue = planes * blocks

    rel_mine = rel[0, 0]
    mine = (rel_mine // inside)[None, :] == jnp.arange(planes, dtype=i32)[:, None]
    mine = jnp.pad(mine, ((0, 0), (0, queue - blocks)))
    column = rel[:, 0, :].reshape(1, queue)
    here = column < inside
    row_of = jnp.arange(queue, dtype=i32)[None, :] // blocks
    per_row = here & (row_of == jnp.arange(planes, dtype=i32)[:, None])
    to_dest = column == jnp.arange(inside, dtype=i32)[:, None]
    to_me = (rel == 0).transpose(1, 0, 2).reshape(inside, queue)
    local_of = local.transpose(1, 0, 2).reshape(inside, queue)
    ranks = earlier(jnp.concatenate([mine, per_row, to_dest, to_me], axis=0))
    rank_mine, rank_row, rank_dest, rank_me = jnp.split(
        ranks, [planes, 2 * planes, 2 * planes + inside]
    )
    rank_row = jnp.sum(jnp.where(per_row, rank_row, 0), axis=0, keepdims=True)

    wet = ocean_mask.reshape(tiles, cells)
    room1 = min(blocks, wide * cap)
    room2 = min(queue, planes * cap)
    slots = inside * room2
    index = jnp.arange(blocks, dtype=i32)
    src1 = pick(mine[:, :blocks], rank_mine[:, :blocks], room1, index).reshape(-1)
    src2 = pick(to_dest, rank_dest, room2, row_of * room1 + rank_row).reshape(-1)
    tile_of = pick(to_me, rank_me, room2, (local_of + 1)[:, None, :]).reshape(-1)
    slot = jnp.arange(slots, dtype=i32)
    alike = (tile_of[:, None] == tile_of[None, :]) & (slot[None, :] < slot[:, None])
    alike = alike & (tile_of[:, None] > 0)
    prev = jnp.min(jnp.where(alike, slots - 1 - slot[None, :], slots), axis=1)
    prev = jnp.where(prev == slots, slots, slots - 1 - prev)
    listed = jnp.arange(tiles, dtype=i32) + 1
    hit = listed[:, None] == tile_of[None, :]
    last = jnp.min(jnp.where(hit, slots - 1 - slot[None, :], slots), axis=1)
    last = jnp.where(last == slots, slots, slots - 1 - last)
    lists = jnp.concatenate([src1, src2, prev, last])

    mean1 = blocks // planes
    mean2 = max(1, queue // everyone)
    rooms = [
        (min(room1, a * mean1 // 16), min(room2, b * mean2 // 16))
        for a, b in ((22, 44), (24, 44), (25, 46), (26, 48), (28, 48))
    ] + [(room1, room2)]

    source = jnp.arange(everyone, dtype=i32).reshape(planes, inside, 1)
    plane_of = ((rel ^ source) // inside).reshape(1, everyone, blocks)
    others = jnp.arange(1, planes, dtype=i32)[:, None, None]
    load1 = jnp.sum((plane_of == others).astype(i32), axis=2).reshape(-1)
    by_column = rel.transpose(1, 0, 2).reshape(inside, 1, queue)
    owners = jnp.arange(everyone, dtype=i32)[None, :, None]
    load2 = jnp.sum((by_column == owners).astype(i32), axis=2).reshape(-1)
    need1 = sum((load1 > a).astype(i32) for a, _ in rooms[:-1])
    need2 = sum((load2 > b).astype(i32) for _, b in rooms[:-1])
    choice = jnp.max(jnp.concatenate([need1, need2]))

    def run(n):
        shape = (bands, halves, planes, room1, room2, *rooms[n], chunks, tiles)
        return exchange(shape, 2 + n, lists, partial, covered, wet)

    return lax.switch(choice, [functools.partial(run, n) for n in range(len(rooms))])


def solution(mesh):
    in_specs = (
        P(None, ("band", "sub")),
        P(("band", "sub"), None, None),
        P(("band", "sub")),
        P(("band", "sub"), None),
        P(("band", "sub")),
        P(("band", "sub")),
    )
    out_specs = P(None, ("band", "sub"))
    return jax.shard_map(
        per_device, mesh=mesh, in_specs=in_specs, out_specs=out_specs, check_vma=False
    )
```

time: 137 us -> 112 us (0.82)
  Pallas kernels: 123 us -> 101 us
  other arithmetic: 8.26 us -> 5.22 us
  local copies, waits for them, and re-layouts: 1.52 us -> 3.12 us
  between operations: 2.95 us -> 1.5 us
    pallas_call x1 -> x0, Pallas kernels: 11.6 us -> none  [gather(): pl.pallas_call(functools.partial(gather_kernel, chunks, tiles), grid=(ins...]
    pallas_call x1, Pallas kernels: 99.2 us -> 88.8 us  [exchange(): pl.pallas_call(functools.partial(exchange_kernel, shape), in_specs=[smem,...]
    unnamed x2 -> x3, local copies, waits for them, and re-layouts: 0.01 us -> 2.8 us
    reduce_sum x2, other arithmetic: 2.02 us -> 0.43 us  [the longest x1 0.22 us: per_device(): load2 = jnp.sum((by_column == owners).astype(i32), axis=2).reshape(-1)]
where the time goes in v2:
time: 112 us; the launch traced here: 111 us
  Pallas kernels  101 us (90%)
  other arithmetic  5.22 us (5%)
  local copies, waits for them, and re-layouts  3.12 us (3%)
  between operations  1.5 us (1%)
    pallas_call x1, Pallas kernels, exchange(): pl.pallas_call(functools.partial(exchange_kernel, shape), in_specs=[smem,...  88.8 us
    pallas_call x1, Pallas kernels, block_products(): pl.pallas_call(functools.partial(block_kernel, group, chunks, bands, halv...  12.1 us
    unnamed x3, local copies, waits for them, and re-layouts  2.8 us

profile of v2, /device:TPU:17, one launch (start us, length us, event | category | flops | bytes accessed | tf_op | source)
XLA Modules:
  0.0 111.2 jit_solution(9724143829573525085)
XLA Ops:
  0.0 0.0 copy-start
  0.0 1.2 %add_bitcast_fusion.t_ref = s32[1,128]{1,0:T(1,128)} fusion(s32[128]{0:T(128)} %param.16, s32[128,1]{0,1:T(1,128)} %param.15), kind=kLoop, calls=%fused_computation.68 | loop fusion | flops 1792 | bytes 1536 | tf_op jit(solution)/shard_map/broadcast_in_dim | solution.py:429
  1.3 0.1 reshape.234
  1.4 12.1 %block_products.1 = (bf16[8,128,8,128]{3,2,1,0:T(8,128)(2,1)S(1)}, f32[128,128]{1,0:T(8,128)S(1)}, s32[32,1,128]{2,1,0:T(1,128)}) custom-call(bf16[64,16384]{1,0:T(8,128)(2,1)} %v_ref.1, bf16[128,128,128]{2,1,0:T(8,128)(2,1)} %w_ref.1, s32[1,16384]{1,0:T(1,128)} %bitcast.46, s32[1,128]{1,0:T(1,128)} %add_bitcast_fusion.t_ref), custom_call_target="tpu_custom_call" | custom-call | tf_op jit(solution)/shard_map/block_products/pallas_call | solution.py:88
  13.5 0.8 and_add_fusion
  14.3 0.2 convert_reduce_fusion
  14.5 0.7 fusion.15
  15.2 0.1 add_select_fusion
  15.3 0.2 convert_reduce_fusion.1
  15.5 0.6 add_reduce_fusion
  17.5 0.2 convolution_convert_fusion
  17.8 0.1 select_reduce_fusion.4
  17.9 0.1 reshape.236
  18.0 0.5 select_reduce_fusion.1
  18.6 0.1 eq.184
  18.6 0.2 select_reduce_fusion.3
  18.9 0.3 select_reduce_fusion
  19.2 0.1 reshape.237
  19.3 0.0 copy-done
  19.3 89.1 %conditional.1 = (f32[64,25600]{1,0:T(8,128)S(1)}) conditional(s32[]{:T(128)} %clamp.3, (s32[1480]{0:T(1024)S(1)}, bf16[8,128,8,128]{3,2,1,0:T(8,128)(2,1)S(1)}, f32[128,128]{1,0:T(8,128)S(1)}, s32[25600]{0:T(1024)S(1)}) %tuple.39, (s32[1480]{0:T(1024)S(1)}, bf16[8,128,8,128]{3,2,1,0:T(8,128)(2,1)S(1)}, ...), branch_computations={%region_10.11_spmd, %region_11.12_spmd, %region_12.13_spmd, %regio... | conditional | bytes 8 | solution.py:494
  19.3 88.8 %exchange.6 = f32[64,25600]{1,0:T(8,128)S(1)} custom-call(s32[1480]{0:T(1024)S(1)} %get-tuple-element.53.list_ref, bf16[8,128,8,128]{3,2,1,0:T(8,128)(2,1)S(1)} %get-tuple-element.54.p_ref, f32[128,128]{1,0:T(8,128)S(1)} %get-tuple-element.60.c_ref, s32[200,128]{1,0:T(8,128)S(1)} %bitcast.35), custom_call_target="tpu_custom_call" | custom-call | tf_op jit(solution)/shard_map/cond/branch_0_fun/exchange/pallas_call | solution.py:360
  108.4 2.8 %copy.26 = f32[64,25600]{1,0:T(8,128)} copy(f32[64,25600]{1,0:T(8,128)S(1)} %get-tuple-element.90) | data formatting | bytes 13107200
  (20 shorter events, 0.1 us)
Async XLA Ops:
  0.0 19.3 %copy-start = (s32[25600]{0:T(1024)S(1)}, s32[25600]{0:T(1024)}, u32[]{:S(2)}) copy-start(s32[25600]{0:T(1024)} %param.17) | copy-start | bytes 307204

commit v3 on v2

--- a/solution.py
+++ b/solution.py
@@ -22,13 +22,27 @@
 
 
 def block_kernel(
-    group, chunks, bands, halves, v_ref, w_ref, m_ref, t_ref, p_ref, c_ref, r_ref,
-    landed, send_sem, recv_sem,
+    group, chunks, bands, halves, tiles, shift,
+    v_ref, w_ref, m_ref, band_ref, tile_ref, p_ref, c_ref, r_ref,
+    values, weights, named, landed, v_sem, w_sem, send_sem, recv_sem,
 ):
     band = lax.axis_index("band")
     half = lax.axis_index("sub")
-    cells = w_ref.shape[1]
+    blocks, cells, _ = weights.shape
     everyone = bands * halves
+    pieces = blocks // group
+
+    def value_copy(i):
+        lanes = pl.ds(pl.multiple_of(i * group * cells, cells), group * cells)
+        return pltpu.make_async_copy(v_ref.at[:, lanes], values.at[:, lanes], v_sem.at[i])
+
+    def weight_copy(i):
+        rows = pl.ds(i * group, group)
+        return pltpu.make_async_copy(w_ref.at[rows], weights.at[rows], w_sem.at[i])
+
+    for i in range(pieces):
+        value_copy(i).start()
+        weight_copy(i).start()
 
     def peer(k):
         return {
@@ -38,80 +52,92 @@
 
     def index_copy(k):
         return pltpu.make_async_remote_copy(
-            src_ref=t_ref, dst_ref=landed.at[k],
+            src_ref=named, dst_ref=landed.at[k],
             send_sem=send_sem.at[k], recv_sem=recv_sem.at[k],
             device_id=peer(k), device_id_type=MESH,
         )
 
-    @pl.when(pl.program_id(0) == 0)
-    def _():
-        barrier = pltpu.get_barrier_semaphore()
-
-        @pl.loop(1, everyone)
-        def _(k):
-            pl.semaphore_signal(barrier, inc=1, device_id=peer(k), device_id_type=MESH)
-
-        pl.semaphore_wait(barrier, everyone - 1)
-
-        @pl.loop(1, everyone)
-        def _(k):
-            index_copy(k).start()
-
-    for j in range(group):
-        lanes = pl.ds(j * cells, cells)
-        mb = m_ref[:, lanes].astype(f32).astype(bf16)
-        lhs = jnp.concatenate(
-            [v_ref[:, lanes] * mb, jnp.broadcast_to(mb, (16, cells))], axis=0
-        )
-        p = jnp.dot(lhs, w_ref[j], preferred_element_type=f32)
-        for c in range(chunks):
-            p_ref[c, j] = p[c * ROWS:(c + 1) * ROWS].astype(bf16)
-        c_ref[pl.ds(j, 1), :] = p[chunks * ROWS:chunks * ROWS + 1].astype(bf16).astype(f32)
-
-    @pl.when(pl.program_id(0) == pl.num_programs(0) - 1)
-    def _():
-        @pl.loop(1, everyone)
-        def _(k):
-            index_copy(k).wait_send()
-            index_copy(k).wait_recv()
-
-        r_ref[0] = t_ref[...]
-        r_ref[pl.ds(1, everyone - 1)] = landed[pl.ds(1, everyone - 1)]
-
-
-def block_products(bands, halves, values, weights, mask, owners):
+    barrier = pltpu.get_barrier_semaphore()
+
+    @pl.loop(1, everyone)
+    def _(k):
+        pl.semaphore_signal(barrier, inc=1, device_id=peer(k), device_id_type=MESH)
+
+    tile = tile_ref[...]
+    side = jnp.zeros_like(tile)
+    for h in range(1, halves):
+        side = side + (tile >= h * tiles).astype(i32)
+    named[...] = (band_ref[...] * halves + side) * (1 << shift) + tile - side * tiles
+
+    def multiply(i):
+        value_copy(i).wait()
+        weight_copy(i).wait()
+        for u in range(group):
+            j = i * group + u
+            lanes = pl.ds(pl.multiple_of(j * cells, cells), cells)
+            mb = m_ref[:, lanes].astype(f32).astype(bf16)
+            lhs = jnp.concatenate(
+                [values[:, lanes] * mb, jnp.broadcast_to(mb, (16, cells))], axis=0
+            )
+            p = jnp.dot(lhs, weights[j], preferred_element_type=f32)
+            for c in range(chunks):
+                p_ref[c, j] = p[c * ROWS:(c + 1) * ROWS].astype(bf16)
+            c_ref[pl.ds(j, 1), :] = p[chunks * ROWS:chunks * ROWS + 1].astype(bf16).astype(f32)
+
+    multiply(0)
+    pl.semaphore_wait(barrier, everyone - 1)
+
+    @pl.loop(1, everyone)
+    def _(k):
+        index_copy(k).start()
+
+    @pl.loop(1, pieces)
+    def _(i):
+        multiply(i)
+
+    @pl.loop(1, everyone)
+    def _(k):
+        index_copy(k).wait_send()
+        index_copy(k).wait_recv()
+
+    r_ref[0] = named[...]
+    r_ref[pl.ds(1, everyone - 1)] = landed[pl.ds(1, everyone - 1)]
+
+
+def block_products(bands, halves, tiles, shift, values, weights, mask, band, tile):
     fields = values.shape[0]
     blocks, cells, out_cells = weights.shape
     chunks = fields // ROWS
     group = 16
+    pieces = blocks // group
     everyone = bands * halves
+    vmem = pl.BlockSpec(memory_space=pltpu.VMEM)
+    hbm = pl.BlockSpec(memory_space=pltpu.HBM)
+    dma = pltpu.SemaphoreType.DMA
     return pl.pallas_call(
-        functools.partial(block_kernel, group, chunks, bands, halves),
-        grid=(blocks // group,),
-        in_specs=[
-            pl.BlockSpec((fields, group * cells), lambda i: (0, i)),
-            pl.BlockSpec((group, cells, out_cells), lambda i: (i, 0, 0)),
-            pl.BlockSpec((1, group * cells), lambda i: (0, i)),
-            pl.BlockSpec(memory_space=pltpu.VMEM),
-        ],
-        out_specs=[
-            pl.BlockSpec((chunks, group, ROWS, out_cells), lambda i: (0, i, 0, 0)),
-            pl.BlockSpec((group, out_cells), lambda i: (i, 0)),
-            pl.BlockSpec(memory_space=pltpu.VMEM),
-        ],
+        functools.partial(block_kernel, group, chunks, bands, halves, tiles, shift),
+        in_specs=[hbm, hbm, vmem, vmem, vmem],
+        out_specs=[vmem, vmem, vmem],
         out_shape=[
             jax.ShapeDtypeStruct((chunks, blocks, ROWS, out_cells), bf16),
             jax.ShapeDtypeStruct((blocks, out_cells), f32),
             jax.ShapeDtypeStruct((everyone, 1, blocks), i32),
         ],
         scratch_shapes=[
+            pltpu.VMEM(values.shape, bf16),
+            pltpu.VMEM(weights.shape, bf16),
+            pltpu.VMEM((1, blocks), i32),
             pltpu.VMEM((everyone, 1, blocks), i32),
-            pltpu.SemaphoreType.DMA((everyone,)),
-            pltpu.SemaphoreType.DMA((everyone,)),
+            dma((pieces,)),
+            dma((pieces,)),
+            dma((everyone,)),
+            dma((everyone,)),
         ],
-        compiler_params=pltpu.CompilerParams(collective_id=1, has_side_effects=True),
+        compiler_params=pltpu.CompilerParams(
+            collective_id=1, has_side_effects=True, vmem_limit_bytes=59 * 1024 * 1024
+        ),
         name="block_products",
-    )(values, weights, mask, owners)
+    )(values, weights, mask, band, tile)
 
 
 def exchange_kernel(
@@ -421,12 +447,9 @@
     inside = wide * halves
     shift = (tiles - 1).bit_length()
 
-    tile = dest_band[:, 0] * (halves * tiles) + dest_tile
-    owner = tile // tiles
-    packed = owner * (1 << shift) + (tile - owner * tiles)
-
     partial, covered, landed = block_products(
-        bands, halves, land_values, area_weights, land_mask[None, :], packed[None, :]
+        bands, halves, tiles, shift, land_values, area_weights,
+        land_mask[None, :], dest_band.reshape(1, blocks), dest_tile[None, :],
     )
 
     landed = landed.reshape(planes, inside, blocks)

time: 112 us -> 114 us (1.018)
  Pallas kernels: 101 us -> 105 us
  other arithmetic: 5.22 us -> 3.99 us
    pallas_call x1, Pallas kernels: 88.8 us -> 93.9 us  [exchange(): pl.pallas_call(functools.partial(exchange_kernel, shape), in_specs=[smem,...]
    broadcast_in_dim x1 -> x0, other arithmetic: 1.23 us -> none  [per_device(): packed[None, :]]
where the time goes in v3:
time: 114 us
  Pallas kernels  105 us (92%)
  other arithmetic  3.99 us (4%)
  local copies, waits for them, and re-layouts  3.12 us (3%)
  between operations  1.51 us (1%)
    pallas_call x1, Pallas kernels, exchange(): pl.pallas_call(functools.partial(exchange_kernel, shape), in_specs=[smem,...  93.9 us
    pallas_call x1, Pallas kernels, block_products(): pl.pallas_call(functools.partial(block_kernel, group, chunks, bands, halv...  11 us
    unnamed x3, local copies, waits for them, and re-layouts  2.8 us

profile of v3, /device:TPU:17, one launch (start us, length us, event | category | flops | bytes accessed | tf_op | source)
XLA Modules:
  0.0 114.1 jit_solution(1090329955234157139)
XLA Ops:
  0.0 0.0 copy-start
  0.0 0.1 reshape.236
  0.1 11.0 %block_products.1 = (bf16[8,128,8,128]{3,2,1,0:T(8,128)(2,1)S(1)}, f32[128,128]{1,0:T(8,128)S(1)}, s32[32,1,128]{2,1,0:T(1,128)}) custom-call(bf16[64,16384]{1,0:T(8,128)(2,1)} %v_ref.1, bf16[128,128,128]{2,1,0:T(8,128)(2,1)} %w_ref.1, s32[1,16384]{1,0:T(1,128)} %bitcast.42, s32[1,128]{1,0:T(1,128)} %bitcast.46, s32[1,128]{1,0:T(1,128)} %bitcast.47), custom_call_target="tpu_custom_call" | custom-call | tf_op jit(solution)/shard_map/block_products/pallas_call | solution.py:117
  11.2 0.8 and_add_fusion
  12.0 0.2 convert_reduce_fusion
  12.2 0.7 fusion.15
  12.9 0.1 add_select_fusion
  13.0 0.2 convert_reduce_fusion.1
  13.2 0.6 add_reduce_fusion
  15.2 0.2 convolution_convert_fusion
  15.5 0.1 select_reduce_fusion.4
  15.6 0.1 reshape.238
  15.7 0.5 select_reduce_fusion.1
  16.3 0.1 eq.184
  16.3 0.2 select_reduce_fusion.3
  16.6 0.3 select_reduce_fusion
  16.9 0.1 reshape.239
  17.0 0.0 copy-done
  17.0 94.3 %conditional.1 = (f32[64,25600]{1,0:T(8,128)S(1)}) conditional(s32[]{:T(128)} %clamp.3, (s32[1480]{0:T(1024)S(1)}, bf16[8,128,8,128]{3,2,1,0:T(8,128)(2,1)S(1)}, f32[128,128]{1,0:T(8,128)S(1)}, s32[25600]{0:T(1024)S(1)}) %tuple.39, (s32[1480]{0:T(1024)S(1)}, bf16[8,128,8,128]{3,2,1,0:T(8,128)(2,1)S(1)}, ...), branch_computations={%region_10.11_spmd, %region_11.12_spmd, %region_12.13_spmd, %regio... | conditional | bytes 8 | solution.py:517
  17.1 93.9 %exchange.7 = f32[64,25600]{1,0:T(8,128)S(1)} custom-call(s32[1480]{0:T(1024)S(1)} %get-tuple-element.64.list_ref, bf16[8,128,8,128]{3,2,1,0:T(8,128)(2,1)S(1)} %get-tuple-element.65.p_ref, f32[128,128]{1,0:T(8,128)S(1)} %get-tuple-element.66.c_ref, s32[200,128]{1,0:T(8,128)S(1)} %bitcast.32), custom_call_target="tpu_custom_call" | custom-call | tf_op jit(solution)/shard_map/cond/branch_1_fun/exchange/pallas_call | solution.py:386
  111.3 2.8 %copy.26 = f32[64,25600]{1,0:T(8,128)} copy(f32[64,25600]{1,0:T(8,128)S(1)} %get-tuple-element.90) | data formatting | bytes 13107200
  (20 shorter events, 0.1 us)
Async XLA Ops:
  0.0 17.0 %copy-start = (s32[25600]{0:T(1024)S(1)}, s32[25600]{0:T(1024)}, u32[]{:S(2)}) copy-start(s32[25600]{0:T(1024)} %param.17) | copy-start | bytes 307204

commit v4 on v3

--- a/solution.py
+++ b/solution.py
@@ -2,6 +2,7 @@
 
 import jax
 import jax.numpy as jnp
+import numpy as np
 from jax import lax
 from jax.experimental import pallas as pl
 from jax.experimental.pallas import tpu as pltpu
@@ -13,11 +14,21 @@
 f32, bf16, i32 = jnp.float32, jnp.bfloat16, jnp.int32
 
 
-def target_of(me, k, size):
-    peer, bit = 0, 1
+def peers_of(me, low, size):
+    steps, bit = [], low
     while bit < size:
-        peer = peer + bit * lax.rem(me // bit + k // bit, 2)
+        steps.append(bit - 2 * bit * lax.rem(me // bit, 2))
         bit *= 2
+
+    def peer(k):
+        index = me
+        for n, step in enumerate(steps):
+            if not isinstance(k, int):
+                index = index + step * lax.rem(k // 2 ** n, 2)
+            elif k // 2 ** n % 2:
+                index = index + step
+        return index
+
     return peer
 
 
@@ -44,11 +55,10 @@
         value_copy(i).start()
         weight_copy(i).start()
 
+    band_at, half_at = peers_of(band, 1, bands), peers_of(half, 1, halves)
+
     def peer(k):
-        return {
-            "band": target_of(band, k // halves, bands),
-            "sub": target_of(half, lax.rem(k, halves), halves),
-        }
+        return {"band": band_at(k // halves), "sub": half_at(k % halves)}
 
     def index_copy(k):
         return pltpu.make_async_remote_copy(
@@ -58,9 +68,7 @@
         )
 
     barrier = pltpu.get_barrier_semaphore()
-
-    @pl.loop(1, everyone)
-    def _(k):
+    for k in range(1, everyone):
         pl.semaphore_signal(barrier, inc=1, device_id=peer(k), device_id_type=MESH)
 
     tile = tile_ref[...]
@@ -86,17 +94,14 @@
 
     multiply(0)
     pl.semaphore_wait(barrier, everyone - 1)
-
-    @pl.loop(1, everyone)
-    def _(k):
+    for k in range(1, everyone):
         index_copy(k).start()
 
     @pl.loop(1, pieces)
     def _(i):
         multiply(i)
 
-    @pl.loop(1, everyone)
-    def _(k):
+    for k in range(1, everyone):
         index_copy(k).wait_send()
         index_copy(k).wait_recv()
 
@@ -143,7 +148,8 @@
 def exchange_kernel(
     shape, list_ref, p_ref, c_ref, wet_ref, out_ref, *scratch
 ):
-    bands, halves, planes, room1, room2, first, second, chunks, tiles = shape
+    bands, halves, planes, room1, room2, firsts, second, chunks, tiles = shape
+    first = max(firsts)
     wide = bands // planes
     inside = wide * halves
     cover1, cover2 = -(-first // 8) * 8, -(-second // 8) * 8
@@ -159,14 +165,15 @@
     at_prev = at2 + slots
     at_last = at_prev + slots
 
+    here = band // wide
+    z_at = peers_of(here, 1, planes)
+    wide_at, half_at = peers_of(band, 1, wide), peers_of(half, 1, halves)
+
     def z_peer(k):
-        return {"band": target_of(band, k * wide, bands)}
+        return {"band": band + (z_at(k) - here) * wide}
 
     def plane_peer(k):
-        return {
-            "band": target_of(band, k // halves, bands),
-            "sub": target_of(half, lax.rem(k, halves), halves),
-        }
+        return {"band": wide_at(k // halves), "sub": half_at(k % halves)}
 
     barrier = pltpu.get_barrier_semaphore()
 
@@ -180,13 +187,26 @@
 
     pl.semaphore_wait(barrier, planes + inside - 2)
 
-    def z_copy(c, k):
+    def z_copy(c, k, size):
         return pltpu.make_async_remote_copy(
-            src_ref=send1.at[c, k],
-            dst_ref=recv1[c].at[pl.ds(k * room1, first)],
+            src_ref=send1.at[c, k, pl.ds(0, size)],
+            dst_ref=recv1[c].at[pl.ds(k * room1, size)],
             send_sem=sem1.at[c, k], recv_sem=rem1.at[c, k],
             device_id=z_peer(k), device_id_type=MESH,
         )
+
+    def each_target(body):
+        for plane in range(planes):
+            @pl.when(here != plane)
+            def _(plane=plane):
+                body(z_at(plane), firsts[plane])
+
+    def each_source(body):
+        for plane in range(planes):
+            @pl.when(here == plane)
+            def _(plane=plane):
+                for k in range(1, planes):
+                    body(k, firsts[plane])
 
     def plane_copy(c, k):
         return pltpu.make_async_remote_copy(
@@ -214,7 +234,7 @@
             done.at[c % 2], out_ref.at[pl.ds(c * ROWS, ROWS), :], out_sem.at[c % 2]
         )
 
-    def each(count, body, step=16):
+    def each(count, body, step=8):
         @pl.loop(0, count // step)
         def _(g):
             for u in range(step):
@@ -230,7 +250,8 @@
                 send1[c, k, j] = p_ref[c, list_ref[k * room1 + j]]
 
             each(first, pack)
-            z_copy(c, k).start()
+
+        each_target(lambda k, size: z_copy(c, k, size).start())
 
         def keep(j):
             recv1[c][j] = p_ref[c, list_ref[j]]
@@ -341,10 +362,7 @@
         send_chunk(c)
 
     for c in range(chunks):
-        @pl.loop(1, planes)
-        def _(k, c=c):
-            z_copy(c, k).wait_recv()
-
+        each_source(lambda k, size: z_copy(c, k, size).wait_recv())
         if c + window < chunks:
             send_chunk(c + window)
         forward_chunk(c)
@@ -361,8 +379,9 @@
     @pl.loop(1, planes)
     def _(k):
         z_cover(k).wait_send()
-        for c in range(chunks):
-            z_copy(c, k).wait_send()
+
+    for c in range(chunks):
+        each_target(lambda k, size: z_copy(c, k, size).wait_send())
 
     @pl.loop(1, inside)
     def _(k):
@@ -375,7 +394,8 @@
 
 
 def exchange(shape, ident, lists, partial, covered, wet):
-    bands, halves, planes, room1, room2, first, second, chunks, tiles = shape
+    bands, halves, planes, room1, room2, firsts, second, chunks, tiles = shape
+    first = max(firsts)
     _, _, rows, cells = partial.shape
     inside = bands * halves // planes
     slots = inside * room2
@@ -494,21 +514,35 @@
 
     mean1 = blocks // planes
     mean2 = max(1, queue // everyone)
+    sizes = [(a,) * planes for a in (44, 48)] if planes != 4 else [
+        (40, 44, 40, 44), (38, 50, 50, 38), (50, 38, 38, 50),
+        (44, 46, 44, 46), (40, 56, 40, 56), (56, 40, 56, 40),
+    ]
     rooms = [
-        (min(room1, a * mean1 // 16), min(room2, b * mean2 // 16))
-        for a, b in ((22, 44), (24, 44), (25, 46), (26, 48), (28, 48))
-    ] + [(room1, room2)]
-
-    source = jnp.arange(everyone, dtype=i32).reshape(planes, inside, 1)
-    plane_of = ((rel ^ source) // inside).reshape(1, everyone, blocks)
-    others = jnp.arange(1, planes, dtype=i32)[:, None, None]
-    load1 = jnp.sum((plane_of == others).astype(i32), axis=2).reshape(-1)
+        (tuple(min(room1, a * mean1 // 32) for a in size), min(room2, b * mean2 // 16))
+        for size, b in [(size, 44) for size in sizes]
+        + [((52,) * planes, 48), ((56,) * planes, 48)]
+    ] + [((room1,) * planes, room2)]
+
+    source = jnp.arange(everyone, dtype=i32).reshape(planes, inside) ^ me
+    plane_of = ((landed >> shift) // inside).reshape(1, everyone, blocks)
+    target = jnp.arange(planes, dtype=i32)[:, None]
+    load1 = jnp.sum((plane_of == target[:, :, None]).astype(i32), axis=2)
+    load1 = jnp.where((source // inside).reshape(1, everyone) == target, 0, load1)
     by_column = rel.transpose(1, 0, 2).reshape(inside, 1, queue)
     owners = jnp.arange(everyone, dtype=i32)[None, :, None]
-    load2 = jnp.sum((by_column == owners).astype(i32), axis=2).reshape(-1)
-    need1 = sum((load1 > a).astype(i32) for a, _ in rooms[:-1])
-    need2 = sum((load2 > b).astype(i32) for _, b in rooms[:-1])
-    choice = jnp.max(jnp.concatenate([need1, need2]))
+    load2 = jnp.sum((by_column == owners).astype(i32), axis=2)
+    need1, need2 = jnp.zeros_like(load1), jnp.zeros_like(load2)
+    for n, (size, b) in enumerate(rooms[:-1]):
+        allowed = sum((target == p).astype(i32) * a for p, a in enumerate(size))
+        need1 = need1 | ((load1 > allowed).astype(i32) << n)
+        need2 = need2 | ((load2 > b).astype(i32) << n)
+    need = jnp.concatenate([need1, need2]) if planes != inside else need1 | need2
+    full = lax.reduce(need, np.int32(0), lax.bitwise_or, (0, 1))
+    choice, still = jnp.int32(0), jnp.int32(1)
+    for n in range(len(rooms) - 1):
+        still = still & (full >> n)
+        choice = choice + still
 
     def run(n):
         shape = (bands, halves, planes, room1, room2, *rooms[n], chunks, tiles)

time: 114 us -> 110 us (0.965)
  the two profiles are of different devices: /device:TPU:17 before, /device:TPU:25 now
where the time goes in v4:
time: 110 us
  Pallas kernels  100 us (91%)
  other arithmetic  3.96 us (4%)
  local copies, waits for them, and re-layouts  3.12 us (3%)
  between operations  1.53 us (1%)
    pallas_call x1, Pallas kernels, exchange(): pl.pallas_call(functools.partial(exchange_kernel, shape), in_specs=[smem,...  90.4 us
    pallas_call x1, Pallas kernels, block_products(): pl.pallas_call(functools.partial(block_kernel, group, chunks, bands, halv...  9.76 us
    unnamed x3, local copies, waits for them, and re-layouts  2.8 us

profile of v4, /device:TPU:25, one launch (start us, length us, event | category | flops | bytes accessed | tf_op | source)
XLA Modules:
  0.0 109.7 jit_solution(5224846729019307300)
XLA Ops:
  0.0 0.0 copy-start
  0.1 0.1 xor.24
  0.2 9.8 %block_products.1 = (bf16[8,128,8,128]{3,2,1,0:T(8,128)(2,1)S(1)}, f32[128,128]{1,0:T(8,128)S(1)}, s32[32,1,128]{2,1,0:T(1,128)}) custom-call(bf16[64,16384]{1,0:T(8,128)(2,1)} %v_ref.1, bf16[128,128,128]{2,1,0:T(8,128)(2,1)} %w_ref.1, s32[1,16384]{1,0:T(1,128)} %bitcast.47, s32[1,128]{1,0:T(1,128)} %bitcast.52, s32[1,128]{1,0:T(1,128)} %bitcast.53), custom_call_target="tpu_custom_call" | custom-call | tf_op jit(solution)/shard_map/block_products/pallas_call | solution.py:122
  10.0 0.8 and_add_fusion
  10.7 0.1 convert_reduce_fusion.1
  10.9 0.7 or_reduce_fusion
  11.7 0.2 convert_reduce_fusion
  11.9 0.7 fusion.17
  14.0 0.2 convolution_convert_fusion
  14.2 0.1 select_reduce_fusion.4
  14.4 0.1 reshape.365
  14.5 0.5 select_reduce_fusion.1
  15.0 0.1 eq.404
  15.1 0.2 select_reduce_fusion.3
  15.3 0.3 select_reduce_fusion
  15.7 0.1 reshape.366
  15.8 0.0 copy-done
  15.8 91.2 %conditional.1 = (f32[64,25600]{1,0:T(8,128)S(1)}) conditional(s32[]{:T(128)} %clamp.3, (s32[1480]{0:T(1024)S(1)}, bf16[8,128,8,128]{3,2,1,0:T(8,128)(2,1)S(1)}, f32[128,128]{1,0:T(8,128)S(1)}, s32[25600]{0:T(1024)S(1)}) %tuple.59, (s32[1480]{0:T(1024)S(1)}, bf16[8,128,8,128]{3,2,1,0:T(8,128)(2,1)S(1)}, ...), branch_computations={%region_10.11_spmd, %region_11.12_spmd, %region_12.13_spmd, %regio... | conditional | bytes 8 | solution.py:551
  16.0 90.4 %exchange.12 = f32[64,25600]{1,0:T(8,128)S(1)} custom-call(s32[1480]{0:T(1024)S(1)} %get-tuple-element.99.list_ref, bf16[8,128,8,128]{3,2,1,0:T(8,128)(2,1)S(1)} %get-tuple-element.100.p_ref, f32[128,128]{1,0:T(8,128)S(1)} %get-tuple-element.101.c_ref, s32[200,128]{1,0:T(8,128)S(1)} %bitcast.37), custom_call_target="tpu_custom_call" | custom-call | tf_op jit(solution)/shard_map/cond/branch_3_fun/exchange/pallas_call | solution.py:406
  106.9 2.8 %copy.35 = f32[64,25600]{1,0:T(8,128)} copy(f32[64,25600]{1,0:T(8,128)S(1)} %get-tuple-element.129) | data formatting | bytes 13107200
  (25 shorter events, 0.2 us)
Async XLA Ops:
  0.0 15.8 %copy-start = (s32[25600]{0:T(1024)S(1)}, s32[25600]{0:T(1024)}, u32[]{:S(2)}) copy-start(s32[25600]{0:T(1024)} %param.20) | copy-start | bytes 307204
